TPU v7x, 32 devices: a whole 2x2x4 slice. The times are simulated.
32 devices in a mesh: fsdp: 32 (over z, y, x, core).
Axes of the slice: x: 2, y: 2, z: 4, core: 2. Of those that a mesh axis runs over, the one named last changes fastest.
Arguments:
- inputs: bfloat16 [256, 197, 384], P('fsdp'), may hold values from -6 to 6
- out_grad: bfloat16 [256, 197, 384], P('fsdp'), may hold values from -6 to 6
- live_counts: int32 [128], P('fsdp'), may hold values from 1 to 2, 192 in all
- norm1_gain: bfloat16 [2, 384], P(None, 'fsdp'), may hold values from 0.5 to 1.5
- norm1_bias: bfloat16 [2, 384], P(None, 'fsdp'), may hold values from -3 to 3
- w_qkv: bfloat16 [2, 384, 1152], P(None, 'fsdp'), may hold values from -0.3125 to 0.3125
- bias_qv: bfloat16 [2, 768], P(None, 'fsdp'), may hold values from -3 to 3
- w_proj: bfloat16 [2, 384, 384], P(None, 'fsdp'), may hold values from -1.25 to 1.25
- bias_proj: bfloat16 [2, 384], P(None, 'fsdp'), may hold values from -3 to 3
- norm2_gain: bfloat16 [2, 384], P(None, 'fsdp'), may hold values from 0.5 to 1.5
- norm2_bias: bfloat16 [2, 384], P(None, 'fsdp'), may hold values from -3 to 3
- w_fc1: bfloat16 [2, 384, 1536], P(None, 'fsdp'), may hold values from -0.3125 to 0.3125
- bias_fc1: bfloat16 [2, 1536], P(None, 'fsdp'), may hold values from -3 to 3
- w_fc2: bfloat16 [2, 1536, 384], P(None, 'fsdp'), may hold values from -0.15625 to 0.15625
- bias_fc2: bfloat16 [2, 384], P(None, 'fsdp'), may hold values from -3 to 3
Outputs:
- outputs: bfloat16 [256, 197, 384], P('fsdp')
- in_grad: float32 [256, 197, 384], P('fsdp')
- grad_norm1_gain: float32 [2, 384], P(None, 'fsdp')
- grad_norm1_bias: float32 [2, 384], P(None, 'fsdp')
- grad_w_qkv: float32 [2, 384, 1152], P(None, 'fsdp')
- grad_bias_qv: float32 [2, 768], P(None, 'fsdp')
- grad_w_proj: float32 [2, 384, 384], P(None, 'fsdp')
- grad_bias_proj: float32 [2, 384], P(None, 'fsdp')
- grad_norm2_gain: float32 [2, 384], P(None, 'fsdp')
- grad_norm2_bias: float32 [2, 384], P(None, 'fsdp')
- grad_w_fc1: float32 [2, 384, 1536], P(None, 'fsdp')
- grad_bias_fc1: float32 [2, 1536], P(None, 'fsdp')
- grad_w_fc2: float32 [2, 1536, 384], P(None, 'fsdp')
- grad_bias_fc2: float32 [2, 384], P(None, 'fsdp')
Inputs may be any that keep to these rules, and one draw needn't show every extreme that they name: `live_counts`: slots at or beyond the count of a micro-batch hold padding.
All inputs are finite; a program needn't handle non-finite values. No bound on the sum of `live_counts` on one device may be relied on, other than what follows from the above.
Results may differ from a plain program's by a relative error of at most 0.012.
Values may be sent and summed in bfloat16 or wider, within the bound.
A program may use at most 256 MiB of HBM per device.

v0:
```python
import functools
import math

import jax
import jax.numpy as jnp
from jax import lax
from jax.experimental import pallas as pl
from jax.experimental.pallas import tpu as pltpu
from jax.sharding import PartitionSpec as P

HEAD_DIM = 64
LAYERS = 2
EPS = 1e-06
BF = jnp.bfloat16
F32 = jnp.float32
NN = (((1,), (0,)), ((), ()))
NT = (((1,), (1,)), ((), ()))
TN = (((0,), (0,)), ((), ()))
KEYS = 256
LANES = 128
VMEM_LIMIT = 67_000_000
PER_STEP = 2
MESH_ID = pl.DeviceIdType.MESH
N1G, N1B, BPJ, BQV, N2G, N2B, BF2, BF1 = range(8)
VECS = 8
ATTN, MLP = 0, 1
COLORS = 2


def torus_shape(devices):
    return {16: (4, 2, 2), 64: (4, 4, 4)}.get(devices // 2, (1, 1, devices // 2))


class Cube:
    def __init__(self, devices):
        self.devices = devices
        self.axes = []
        stride = devices
        for extent in torus_shape(devices):
            stride //= extent
            if extent > 1:
                self.axes.append((extent, stride))
        by_axis, self.bits = [], 0
        for extent, _ in self.axes:
            count = extent.bit_length() - 1
            by_axis.append(list(range(self.bits, self.bits + count)))
            self.bits += count
        self.slots = 1 << self.bits
        orders = [by_axis, by_axis[:1] + by_axis[:0:-1]]
        self.orders = [sum(order, []) for order in orders]

    def bits_of(self, device):
        bits = []
        for extent, stride in self.axes:
            pos = (device // stride) % extent
            bits += [pos // 2, (pos + pos // 2) % 2] if extent == 4 else [pos]
        return bits

    def order(self, color, step):
        return self.orders[color][step]

    def flat(self, color, bits, first=0):
        return sum(bits[self.order(color, s)] * (1 << s) for s in range(first, self.bits))

    def place(self, color, device):
        return device % 2, color, self.flat(color, self.bits_of(device))

    def position(self):
        me = lax.axis_index("fsdp")
        partners = []
        for extent, stride in self.axes:
            pos = (me // stride) % extent
            if extent == 4:
                partners += [me + (3 - 2 * pos) * stride, me + (1 - 2 * (pos % 2)) * stride]
            else:
                partners += [me + (1 - 2 * pos) * stride]
        return self.bits_of(me), me % 2, partners, me + 1 - 2 * (me % 2)


def greet(partners):
    barrier = pltpu.get_barrier_semaphore()
    for partner in partners:
        pl.semaphore_signal(barrier, inc=1, device_id=(partner,), device_id_type=MESH_ID)
    pl.semaphore_wait(barrier, len(partners))


class Group:
    def __init__(self, cube, shapes, sizes):
        self.cube, self.sizes = cube, sizes
        self.rows = min(rows for rows, _ in shapes)
        units = [
            (a, q, c) for a, (rows, lanes) in enumerate(shapes) for c in range(lanes // LANES) for q in range(rows // self.rows)
        ]
        share = -(-len(units) // COLORS)
        self.units = [(i // share, i % share * self.rows, *unit) for i, unit in enumerate(units)]
        self.vec_row = share * self.rows
        self.vec_row += self.vec_row % 2
        self.height = -(-(self.vec_row + (VECS if sizes else 0)) // 16) * 16
        self.pack = 16 // math.gcd(self.rows, 16)

    @property
    def block(self):
        return (COLORS, self.height, LANES)

    @property
    def buffer(self):
        return (2, COLORS, self.cube.slots, self.height, LANES)

    def runs(self):
        return [(i, i + 1 if i % 4 == 3 else i + 3, self.sizes[i]) for i in (0, 3, 4, 7)]

    def pack_own(self, layer, weights, vectors, temp, store):
        for color, row, a, q, c in self.units:
            lanes = slice(c * LANES, (c + 1) * LANES)
            store(color, row, row + self.rows, weights[a][layer, q * self.rows : (q + 1) * self.rows, lanes])
        if self.sizes:
            for i, vector in enumerate(vectors):
                temp[i : i + 1, : vector.shape[1]] = vector[layer : layer + 1, :].astype(F32)
            store(0, self.vec_row, self.vec_row + VECS, temp[...].astype(BF))

    def place(self, color, first, i):
        return self.cube.place(color, first + i)

    def spread(self, buf, targets, vec):
        merged = self.rows % 4 == 0

        def natural(g, _):
            first = g * self.pack
            for a, target in enumerate(targets):
                rows = target.shape[0] // self.cube.devices
                pieces = rows // self.rows
                count = self.pack
                by_lane = {}
                for color, row, b, q, c in self.units:
                    if b == a:
                        by_lane.setdefault(c, {})[q] = (color, row)
                for c, places in by_lane.items():
                    parts = []
                    for i in range(count):
                        for q in range(pieces):
                            color, row = places[q]
                            part = buf[self.place(color, first, i) + (slice(row, row + self.rows), slice(None))]
                            parts.append(part if merged else part.astype(F32))
                    value = jnp.concatenate(parts, axis=0).astype(target.dtype)
                    height = count * rows
                    target[pl.ds(pl.multiple_of(g * height, 16), height), c * LANES : (c + 1) * LANES] = value
            return 0

        lax.fori_loop(0, self.cube.devices // self.pack, natural, 0)
        for d in range(self.cube.devices if self.sizes else 0):
            value = buf[self.place(0, d, 0) + (slice(self.vec_row, self.vec_row + VECS), slice(None))].astype(F32)
            for lo, hi, size in self.runs():
                vec[lo:hi, d * size : (d + 1) * size] = value[lo:hi, :size]

    def split(self, sources, vec, temp, buf):
        merged = self.rows % 4 == 0

        def natural(g, _):
            first = g * self.pack
            for color, row, a, q, c in self.units:
                rows = sources[a].shape[0] // self.cube.devices
                height = self.pack * rows
                value = sources[a][pl.ds(pl.multiple_of(g * height, 16), height), c * LANES : (c + 1) * LANES]
                if not merged:
                    value = value.astype(F32)
                for i in range(self.pack):
                    lo = i * rows + q * self.rows
                    buf[self.place(color, first, i) + (slice(row, row + self.rows), slice(None))] = value[lo : lo + self.rows].astype(BF)
            return 0

        lax.fori_loop(0, self.cube.devices // self.pack, natural, 0)
        for d in range(self.cube.devices if self.sizes else 0):
            for lo, hi, size in self.runs():
                temp[lo:hi, :size] = vec[lo:hi, d * size : (d + 1) * size]
            buf[self.place(0, d, 0) + (slice(self.vec_row, self.vec_row + VECS), slice(None))] = temp[...].astype(BF)

    def emit(self, layer, block, weights, vectors):
        for color, row, a, q, c in self.units:
            lanes = slice(c * LANES, (c + 1) * LANES)
            weights[a][layer, q * self.rows : (q + 1) * self.rows, lanes] = block[color, row : row + self.rows, :]
        for i, vector in enumerate(vectors):
            vector[layer : layer + 1, :] = block[0, self.vec_row + i : self.vec_row + i + 1, : vector.shape[1]]


class Gather:
    def __init__(self, group, position, source, buf, send, recv):
        self.cube, self.group = group.cube, group
        self.mine, self.core, self.partners, self.other = position
        self.source, self.buf, self.send, self.recv = source, buf, send, recv
        self.ticks = self.cube.bits + 2

    @staticmethod
    def semaphores(cube):
        return (COLORS * cube.bits + 1,)

    def copy(self, color, step):
        cube = self.cube
        if step == cube.bits:
            key, partner = COLORS * cube.bits, self.other
            src = dst = self.buf.at[self.core]
        else:
            key, partner = color * cube.bits + step, self.partners[cube.order(color, step)]
            dst = self.buf.at[self.core, color, pl.ds(cube.flat(color, self.mine, step), 1 << step)]
            src = self.source.at[pl.ds(color, 1)] if step == 0 else dst
        return pltpu.make_async_remote_copy(
            src_ref=src,
            dst_ref=dst,
            send_sem=self.send.at[key],
            recv_sem=self.recv.at[key],
            device_id=(partner,),
            device_id_type=MESH_ID,
        )

    def local(self, sem):
        return [
            pltpu.make_async_copy(
                self.source.at[pl.ds(c, 1)], self.buf.at[self.core, c, pl.ds(self.cube.flat(c, self.mine), 1)], sem.at[c]
            )
            for c in range(COLORS)
        ]

    def tick(self, t):
        bits = self.cube.bits
        for color in range(COLORS):
            if 0 < t <= bits:
                self.copy(color, t - 1).wait_recv()
            if t < bits:
                self.copy(color, t).start()
        if t == bits:
            self.copy(0, bits).start()
        if t > bits:
            self.copy(0, bits).wait()
            for color in range(COLORS):
                for step in range(bits):
                    self.copy(color, step).wait_send()


class Scatter:
    def __init__(self, group, position, blocks, inbox, out, send, recv):
        self.cube = group.cube
        self.mine, self.core, self.partners, self.other = position
        self.blocks, self.inbox, self.out, self.send, self.recv = blocks, inbox, out, send, recv
        self.ticks = self.cube.bits + 2

    @staticmethod
    def semaphores(cube):
        return (COLORS * cube.bits + 1,)

    def copy(self, color, step):
        cube = self.cube
        if step == cube.bits:
            key, partner = COLORS * cube.bits, self.other
            src, dst = self.blocks.at[1 - self.core], self.inbox.at[0]
        else:
            key, partner = color * cube.bits + step, self.partners[cube.order(color, step)]
            size = 1 << step
            start = cube.flat(color, self.mine, step) + (1 - 2 * self.mine[cube.order(color, step)]) * size
            src = self.blocks.at[self.core, color, pl.ds(start, size)]
            dst = self.inbox.at[1, color, pl.ds(size, size)]
        return pltpu.make_async_remote_copy(
            src_ref=src,
            dst_ref=dst,
            send_sem=self.send.at[key],
            recv_sem=self.recv.at[key],
            device_id=(partner,),
            device_id_type=MESH_ID,
        )

    def absorb(self, color, step):
        cube = self.cube
        if step == cube.bits:
            start, size, base, box = 0, cube.slots, 0, 0
        else:
            start, size, base, box = cube.flat(color, self.mine, step), 1 << step, 1 << step, 1
        if step == 0:
            self.out[color] = self.blocks[self.core, color, start].astype(F32) + self.inbox[box, color, base].astype(F32)
            return

        def body(j, _):
            at = (self.core, color, start + j)
            self.blocks[at] = self.blocks[at] + self.inbox[box, color, base + j]
            return 0

        lax.fori_loop(0, size, body, 0)

    def tick(self, t):
        bits = self.cube.bits
        if t == 0:
            self.copy(0, bits).start()
            return
        if t == 1:
            self.copy(0, bits).wait_recv()
        for color in range(COLORS):
            if t > 1:
                self.copy(color, bits + 1 - t).wait_recv()
            self.absorb(color, bits + 1 - t)
            if t <= bits:
                self.copy(color, bits - t).start()
        if t == bits + 1:
            self.copy(0, bits).wait_send()
            for color in range(COLORS):
                for step in range(bits):
                    self.copy(color, step).wait_send()


class Rider:
    def __init__(self):
        self.due = {}

    def add(self, step, point, run):
        self.due.setdefault((step, point), []).append(run)

    def at(self, index, point, where=lambda step: True):
        for (step, slot), runs in sorted(self.due.items(), key=lambda item: item[0]):
            if slot == point and where(step):

                @pl.when(index == step)
                def _(runs=runs):
                    for run in runs:
                        run()


def mm(left, right, dims):
    return lax.dot_general(left, right, dims, preferred_element_type=F32)


def norm_stats(hidden):
    centered = hidden - jnp.mean(hidden, axis=-1, keepdims=True)
    inv_std = lax.rsqrt(jnp.mean(centered * centered, axis=-1, keepdims=True) + EPS)
    return centered * inv_std, inv_std


def norm_back(grad_in, normed, inv_std, gain):
    dnorm = grad_in * gain
    return inv_std * (
        dnorm
        - jnp.mean(dnorm, axis=-1, keepdims=True)
        - normed * jnp.mean(dnorm * normed, axis=-1, keepdims=True)
    )


def half_masks():
    lane = lax.broadcasted_iota(jnp.int32, (1, LANES), 1)
    low = (lane < HEAD_DIM).astype(F32).astype(BF)
    return low, 1 - low


class Dims:
    def __init__(self, images, counts, seq, width, ff):
        self.images, self.slots, self.seq, self.width, self.ff = images, images // counts, seq, width, ff
        self.rows = -(-seq // 16) * 16
        self.steps = images // PER_STEP
        self.blk = PER_STEP * self.rows
        self.tot = images * self.rows
        self.flat = images * seq


def vrow(vec_ref, row, width, start=0):
    return vec_ref[row : row + 1, start : start + width]


def image_rows(dims, image):
    return pl.ds(image, dims.seq, stride=dims.images)


def wide_shape(dims):
    return (dims.width // LANES, dims.flat, LANES)


def wide_load(wide, ref):
    for c in range(wide.shape[0]):
        wide[c] = ref[:, c * LANES : (c + 1) * LANES].astype(F32)


def image_get(dims, wide, image):
    return jnp.concatenate([wide[c, image_rows(dims, image), :] for c in range(wide.shape[0])], axis=1)


def image_put(dims, wide, image, value):
    for c in range(wide.shape[0]):
        wide[c, image_rows(dims, image), :] = value[:, c * LANES : (c + 1) * LANES]


def alive(counts, dims, group, slot):
    return jnp.clip(counts[group] - slot, 0, 1).astype(F32)


def fwd_attn_compute(dims, base, vec_ref, wqkv_ref, wproj_ref, outs, scratch):
    n1_ref, inv_ref, qkv_out, e_ref, il_ref, ctx_ref = outs
    stream, qkv_ref = scratch
    width, rows, seq, total = dims.width, dims.rows, dims.seq, dims.blk
    span = pl.ds(base, total)
    h = stream[span, :]
    n1, inv1 = norm_stats(h)
    n1_ref[...] = n1.astype(BF)
    inv_ref[...] = jnp.broadcast_to(inv1, inv_ref.shape)
    attn_in = (n1 * vrow(vec_ref, N1G, width) + vrow(vec_ref, N1B, width)).astype(BF)
    q = (mm(attn_in, wqkv_ref[:, :width], NN) + vrow(vec_ref, BQV, width)).astype(BF) * BF(HEAD_DIM ** -0.5)
    k = mm(attn_in, wqkv_ref[:, width : 2 * width], NN).astype(BF)
    v = (mm(attn_in, wqkv_ref[:, 2 * width :], NN) + vrow(vec_ref, BQV, width, width)).astype(BF)
    for i, part in enumerate((q, k, v)):
        qkv_ref[0:total, i * width : (i + 1) * width] = part
        qkv_out[:, i * width : (i + 1) * width] = part
    low, high = half_masks()
    lane = lax.broadcasted_iota(jnp.int32, (1, KEYS), 1)
    key_mask = jnp.where(lane < seq, 0.0, -1e30).astype(F32)
    lane_low = lax.broadcasted_iota(jnp.int32, (1, LANES), 1) < HEAD_DIM
    ones = jnp.ones((KEYS, LANES), BF)
    for g in range(PER_STEP):
        r0 = g * rows
        for pair in range(width // LANES):
            c0 = pair * LANES
            qp = qkv_ref[r0 : r0 + rows, c0 : c0 + LANES]
            kp = qkv_ref[r0 : r0 + KEYS, width + c0 : width + c0 + LANES]
            vp = qkv_ref[r0 : r0 + KEYS, 2 * width + c0 : 2 * width + c0 + LANES]
            vo = jnp.concatenate([vp, ones], axis=1)
            parts = []
            for half, mask in enumerate((low, high)):
                s = mm(qp * mask, kp, NT) + key_mask
                e = jnp.exp(s - jnp.max(s, axis=-1, keepdims=True)).astype(BF)
                j = 2 * pair + half
                e_ref[r0 : r0 + rows, j * KEYS : (j + 1) * KEYS] = e
                r = mm(e, vo, NN)
                recip = 1.0 / r[:, LANES:]
                parts.append((r[:, :LANES] * recip, recip))
            ctx_ref[r0 : r0 + rows, c0 : c0 + LANES] = jnp.where(lane_low, parts[0][0], parts[1][0]).astype(BF)
            il_ref[r0 : r0 + rows, c0 : c0 + LANES] = jnp.where(lane_low, parts[0][1], parts[1][1])
    stream[span, :] = h + mm(ctx_ref[...], wproj_ref[...], NN) + vrow(vec_ref, BPJ, width)


def fwd_mlp_compute(dims, base, vec_ref, w1_ref, w2_ref, outs, stream):
    n2_ref, inv_ref, act_ref, slope_ref = outs
    width, span = dims.width, pl.ds(base, dims.blk)
    mid = stream[span, :]
    n2, inv2 = norm_stats(mid)
    n2_ref[...] = n2.astype(BF)
    inv_ref[...] = jnp.broadcast_to(inv2, inv_ref.shape)
    mlp_in = (n2 * vrow(vec_ref, N2G, width) + vrow(vec_ref, N2B, width)).astype(BF)
    chunk = 256
    for c in range(0, dims.ff, chunk):
        pre = mm(mlp_in, w1_ref[:, c : c + chunk], NN) + vrow(vec_ref, BF1, chunk, c)
        cdf = 0.5 + 0.5 * lax.erf(pre * 0.7071067811865476)
        act_ref[:, c : c + chunk] = (pre * cdf).astype(BF)
        slope_ref[:, c : c + chunk] = (cdf + pre * jnp.exp(-0.5 * pre * pre) * 0.3989422804014327).astype(BF)
    stream[span, :] = mid + mm(act_ref[...], w2_ref[...], NN) + vrow(vec_ref, BF2, width)


def bwd_mlp_compute(dims, step, poll, vec_ref, w1_ref, w2_ref, saved, scratch, group, blocks):
    n2_ref, inv_ref, act_ref, slope_ref = saved
    stream, thin, act_all, dpre_all, vecs_ref, temp, dw_ref, dw2_ref, _ = scratch
    width, total = dims.width, dims.blk
    gb_all, mlp_all = thin.at[0], thin.at[1]
    span = pl.ds(pl.multiple_of(step * total, 16), total)

    @pl.when(step == 0)
    def _():
        vecs_ref[...] = jnp.zeros_like(vecs_ref)

    gh = stream[span, :]
    gb = gh.astype(BF)
    gb_all[span, :] = gb
    act_all[span, :] = act_ref[...]
    vecs_ref[BF2 : BF2 + 1, :width] += jnp.sum(gh, axis=0, keepdims=True)
    chunk = 256
    for c in range(0, dims.ff, chunk):
        dpre = mm(gb, w2_ref[c : c + chunk, :], NT) * slope_ref[:, c : c + chunk].astype(F32)
        vecs_ref[BF1 : BF1 + 1, c : c + chunk] += jnp.sum(dpre, axis=0, keepdims=True)
        dpre_all[span, c : c + chunk] = dpre.astype(BF)
    poll()
    dmlp = mm(dpre_all[span, :], w1_ref[...], NT)
    n2 = n2_ref[...].astype(F32)
    mlp_all[span, :] = (n2 * vrow(vec_ref, N2G, width) + vrow(vec_ref, N2B, width)).astype(BF)
    vecs_ref[N2G : N2G + 1, :width] += jnp.sum(dmlp * n2, axis=0, keepdims=True)
    vecs_ref[N2B : N2B + 1, :width] += jnp.sum(dmlp, axis=0, keepdims=True)
    gm = gh + norm_back(dmlp, n2, inv_ref[:, 0:1], vrow(vec_ref, N2G, width))
    vecs_ref[BPJ : BPJ + 1, :width] += jnp.sum(gm, axis=0, keepdims=True)
    stream[span, :] = gm

    @pl.when(step == dims.steps - 1)
    def _():
        for c in range(0, dims.ff, 512):
            dw_ref[:, c : c + 512] = mm(mlp_all[...], dpre_all[:, c : c + 512], TN).astype(BF)
            dw2_ref[c : c + 512, :] = mm(act_all[:, c : c + 512], gb_all[...], TN).astype(BF)
        blocks(lambda buf: group.split([dw_ref, dw2_ref], None, temp, buf))


def bwd_attn_compute(dims, step, poll, vec_ref, wqkv_ref, wproj_ref, saved, scratch, group, blocks):
    n1_ref, inv_ref, qkv_in, e_ref, il_ref, ctx_ref = saved
    stream, thin, several, dqkv_all, vecs_ref, temp, dw_ref, _, qkv_ref = scratch
    width, rows, total = dims.width, dims.rows, dims.blk
    gmb_all, ctx_all = thin.at[0], thin.at[1]
    base = pl.multiple_of(step * total, 16)
    span = pl.ds(base, total)
    qkv_ref[0:total, :] = qkv_in[...]
    gm = stream[span, :]
    gmb = gm.astype(BF)
    gmb_all[span, :] = gmb
    ctx_all[span, :] = ctx_ref[...]
    dctx = mm(gmb, wproj_ref[...], NT).astype(BF).astype(F32) * il_ref[...]
    dos_all = dctx.astype(BF)
    doo = dos_all.astype(F32) * ctx_ref[...].astype(F32)
    doo_high = doo.astype(BF)
    doo_low = doo - doo_high.astype(F32)
    lane_low = lax.broadcasted_iota(jnp.int32, (1, LANES), 1) < HEAD_DIM
    low, high = half_masks()
    minus = jnp.full((KEYS, LANES), -1.0, BF)
    for g in range(PER_STEP):
        r0 = g * rows
        rr = pl.ds(pl.multiple_of(base + r0, 16), rows)
        for pair in range(width // LANES):
            c0 = pair * LANES
            qp = qkv_ref[r0 : r0 + rows, c0 : c0 + LANES]
            kp = qkv_ref[r0 : r0 + KEYS, width + c0 : width + c0 + LANES]
            vp = qkv_ref[r0 : r0 + KEYS, 2 * width + c0 : 2 * width + c0 + LANES]
            vm = jnp.concatenate([vp, minus], axis=1)
            dos = dos_all[r0 : r0 + rows, c0 : c0 + LANES]
            upper = doo_high[r0 : r0 + rows, c0 : c0 + LANES].astype(F32)
            lower = pltpu.roll(doo_low[r0 : r0 + rows, c0 : c0 + LANES], HEAD_DIM, 1)
            dots = [jnp.where(lane_low, a, b).astype(BF) for a, b in ((upper, lower), (lower, upper))]
            dq = dk = dv = None
            for half, mask in enumerate((low, high)):
                j = 2 * pair + half
                e = e_ref[r0 : r0 + rows, j * KEYS : (j + 1) * KEYS]
                dd = mm(jnp.concatenate([dos * mask, dots[half]], axis=1), vm, NT)
                ds = (e.astype(F32) * dd).astype(BF)
                dv_h = mm(e, dos * mask, TN)
                dk_h = mm(ds, qp * mask, TN)
                dq_h = mm(ds, kp * mask, NN)
                dq = dq_h if dq is None else dq + dq_h
                dk = dk_h if dk is None else dk + dk_h
                dv = dv_h if dv is None else dv + dv_h
            dq = dq * (HEAD_DIM ** -0.5)
            dv = dv[:rows]
            vecs_ref[BQV : BQV + 1, c0 : c0 + LANES] += jnp.sum(dq, axis=0, keepdims=True)
            vecs_ref[BQV : BQV + 1, width + c0 : width + c0 + LANES] += jnp.sum(dv, axis=0, keepdims=True)
            dqkv_all[rr, c0 : c0 + LANES] = dq.astype(BF)
            dqkv_all[rr, width + c0 : width + c0 + LANES] = dk[:rows].astype(BF)
            dqkv_all[rr, 2 * width + c0 : 2 * width + c0 + LANES] = dv.astype(BF)
    poll()
    dai = mm(dqkv_all[span, : 3 * width], wqkv_ref[...], NT)
    n1 = n1_ref[...].astype(F32)
    several[span, :width] = (n1 * vrow(vec_ref, N1G, width) + vrow(vec_ref, N1B, width)).astype(BF)
    vecs_ref[N1G : N1G + 1, :width] += jnp.sum(dai * n1, axis=0, keepdims=True)
    vecs_ref[N1B : N1B + 1, :width] += jnp.sum(dai, axis=0, keepdims=True)
    stream[span, :] = gm + norm_back(dai, n1, inv_ref[:, 0:1], vrow(vec_ref, N1G, width))

    @pl.when(step == dims.steps - 1)
    def _():
        for c in range(0, 3 * width, width):
            dw_ref[:, c : c + width] = mm(several[:, :width], dqkv_all[:, c : c + width], TN).astype(BF)
        dw_ref[:, 3 * width : 4 * width] = mm(ctx_all[...], gmb_all[...], TN).astype(BF)
        blocks(lambda buf: group.split([dw_ref.at[:, : 3 * width], dw_ref.at[:, 3 * width : 4 * width]], vecs_ref, temp, buf))


ANY = pl.BlockSpec(memory_space=pl.ANY)
VM = pl.BlockSpec(memory_space=pltpu.VMEM)
SM = pl.BlockSpec(memory_space=pltpu.SMEM)
SDS = jax.ShapeDtypeStruct
DMA = pltpu.SemaphoreType.DMA


def full(shape):
    return pl.BlockSpec(shape, lambda i: (0,) * len(shape), pipeline_mode=pl.Buffered(1))


def take(refs, *counts):
    refs, parts = list(refs), []
    for count in counts:
        parts.append(refs[:count])
        refs = refs[count:]
    assert not refs
    return parts


def params_of(collective=None):
    extra = {} if collective is None else {"collective_id": collective, "has_side_effects": True}
    return pltpu.CompilerParams(vmem_limit_bytes=VMEM_LIMIT, **extra)


def weight_shapes(dims):
    return [(dims.width, 3 * dims.width), (dims.width, dims.width), (dims.width, dims.ff), (dims.ff, dims.width)]


def forward(cube, dims, groups, live, x, params):
    steps, width, ff, tot = dims.steps, dims.width, dims.ff, dims.tot
    shapes = weight_shapes(dims)
    jobs = [(layer, half) for layer in range(LAYERS) for half in (ATTN, MLP)]
    heads = (width // HEAD_DIM) * KEYS
    saved_attn = [(width, BF), (LANES, F32), (3 * width, BF), (heads, BF), (width, F32), (width, BF)]
    saved_mlp = [(width, BF), (LANES, F32), (ff, BF), (ff, BF)]
    last = 2 * LAYERS * steps - 1

    def body(*refs):
        (live_ref, x_ref), args, (wide,), whole, attn_outs, mlp_outs, scratch, gathers = take(
            refs, 2, 12, 1, 5, len(saved_attn), len(saved_mlp), 10, 4 * len(jobs)
        )
        (n1g, n1b, wqkv, bqv, wproj, bpj, n2g, n2b, w1, bf1, w2, bf2) = args
        temp, local_sem, out_sem, stream, qkv_ref, *kept = scratch
        vec_s, wqkv_s, wproj_s, w1_s, w2_s = kept
        index = pl.program_id(0)
        layer, half, step = index // (2 * steps), (index // steps) % 2, index % steps
        base = pl.multiple_of(step * dims.blk, 16)
        position = cube.position()
        weights = ([wqkv, wproj], [w1, w2])
        vectors = ((n1g, n1b, bpj, bqv, n2g, n2b, bf2, bf1), ())
        works = []
        for n, (job_layer, job_half) in enumerate(jobs):
            own, buf, send, recv = gathers[4 * n : 4 * n + 4]
            works.append(Gather(groups[job_half], position, own, buf, send, recv))
        ticks = works[0].ticks

        def pack(n):
            job_layer, job_half = jobs[n]
            own = gathers[4 * n]

            def store(color, lo, hi, value):
                own[color, lo:hi, :] = value

            own[...] = jnp.zeros_like(own)
            groups[job_half].pack_own(job_layer, weights[job_half], vectors[job_half], temp, store)

        def stage(t):
            for n, work in enumerate(works):
                if 0 <= t - n < ticks:
                    if t == n:
                        for copy in work.local(local_sem.at[n]):
                            copy.start()
                    if t - n == 1:
                        for copy in work.local(local_sem.at[n]):
                            copy.wait()
                    work.tick(t - n)

        def saves(n):
            job_layer, job_half = jobs[n]
            which = (1, 2, 0) if job_half == ATTN else (3, 4)
            return [
                pltpu.make_async_copy(kept[k].at[job_layer], whole[k].at[job_layer], out_sem.at[job_layer, k]) for k in which
            ]

        def finish(n):
            job_layer, job_half = jobs[n]
            targets = [wqkv_s, wproj_s] if job_half == ATTN else [w1_s, w2_s]
            if job_half == ATTN:
                vec_s[job_layer] = jnp.zeros(vec_s.shape[1:], F32)
            groups[job_half].spread(gathers[4 * n + 1], [t.at[job_layer] for t in targets], vec_s.at[job_layer])
            for copy in saves(n):
                copy.start()

        def begin():
            temp[...] = jnp.zeros_like(temp)
            pack(0)
            greet(position[2] + [position[3]])
            for t in range(ticks):
                if 0 < t < len(jobs):
                    pack(t)
                stage(t)
                if t == 2:
                    qkv_ref[dims.blk :, :] = jnp.zeros_like(qkv_ref[dims.blk :, :])
                    stream[...] = jnp.zeros_like(stream)
                    wide_load(wide, x_ref)
                    for image in range(dims.images):
                        stream[image * dims.rows : image * dims.rows + dims.seq, :] = image_get(dims, wide, image)
            finish(0)

        rider = Rider()
        rider.add(0, 0, begin)
        for late in range(1, len(jobs)):
            rider.add(min(late, steps - 1), 0, lambda late=late: stage(ticks + late - 1))
        for n in range(1, len(jobs)):
            rider.add(n * steps, 0, lambda n=n: finish(n))
        rider.at(index, 0)

        @pl.when(half == ATTN)
        def _():
            fwd_attn_compute(
                dims, base, vec_s.at[layer], wqkv_s.at[layer], wproj_s.at[layer], attn_outs, (stream, qkv_ref)
            )

        @pl.when(half == MLP)
        def _():
            fwd_mlp_compute(dims, base, vec_s.at[layer], w1_s.at[layer], w2_s.at[layer], mlp_outs, stream)

        @pl.when(index > last - steps)
        def _():
            for g in range(PER_STEP):
                start = pl.multiple_of(base + g * dims.rows, 16)
                group, slot = step * (PER_STEP // dims.slots) + g // dims.slots, g % dims.slots
                image_put(dims, wide, step * PER_STEP + g, stream[pl.ds(start, dims.seq), :] * alive(live_ref, dims, group, slot))

        @pl.when(index == last)
        def _():
            for n in range(len(jobs)):
                for copy in saves(n):
                    copy.wait()

    sem = DMA(Gather.semaphores(cube))
    lead = lambda i: (i // (2 * steps)) * steps
    half_of = lambda i: (i // steps) % 2
    attn_spec = lambda n: pl.BlockSpec((dims.blk, n), lambda i: (lead(i) + (i % steps) * (1 - half_of(i)) + (steps - 1) * half_of(i), 0))
    mlp_spec = lambda n: pl.BlockSpec((dims.blk, n), lambda i: (lead(i) + (i % steps) * half_of(i), 0))
    whole_shapes = [(LAYERS, VECS, ff)] + [(LAYERS,) + s for s in shapes]
    whole_types = [F32, BF, BF, BF, BF]
    outs = pl.pallas_call(
        body,
        grid=(last + 1,),
        in_specs=[SM, full(x.shape)] + [full(p.shape) for p in params],
        out_specs=[full(wide_shape(dims))]
        + [ANY] * 5
        + [attn_spec(n) for n, _ in saved_attn]
        + [mlp_spec(n) for n, _ in saved_mlp],
        out_shape=[SDS(wide_shape(dims), F32)]
        + [SDS(s, t) for s, t in zip(whole_shapes, whole_types)]
        + [SDS((LAYERS * tot, n), t) for n, t in saved_attn + saved_mlp],
        scratch_shapes=[
            pltpu.VMEM((VECS, LANES), F32),
            DMA((len(jobs), COLORS)),
            DMA((LAYERS, 5)),
            pltpu.VMEM((tot, width), F32),
            pltpu.VMEM((dims.blk + KEYS - dims.rows, 3 * width), BF),
        ]
        + [pltpu.VMEM(s, t) for s, t in zip(whole_shapes, whole_types)]
        + sum([[pltpu.VMEM(groups[h].block, BF), pltpu.VMEM(groups[h].buffer, BF), sem, sem] for _, h in jobs], []),
        compiler_params=params_of(0),
        name="forward",
    )(live, x, *params)
    return outs[0], outs[1:6], outs[6:12], outs[12:16]


def spread_ticks(ticks, polls):
    return polls if ticks == len(polls) else [polls[t * len(polls) // ticks] for t in range(ticks)]


def backward(cube, dims, groups, live, grad, whole, saved_attn, saved_mlp):
    steps, width, ff, tot = dims.steps, dims.width, dims.ff, dims.tot
    jobs = [(layer, half) for layer in reversed(range(LAYERS)) for half in (MLP, ATTN)]
    last = len(jobs) * steps - 1

    def body(*refs):
        (live_ref, og_ref), whole_in, attn_in, mlp_in, (wide,), sums, scratch, kept, scatters = take(
            refs, 2, 5, 6, 4, 1, len(jobs), 10, 5, 4 * len(jobs)
        )
        *work_scratch, load_sem = scratch
        stream, qkv_ref = work_scratch[0], work_scratch[8]
        vec_s, wqkv_s, wproj_s, w1_s, w2_s = kept
        index = pl.program_id(0)
        layer, half, step = LAYERS - 1 - index // (2 * steps), 1 - (index // steps) % 2, index % steps
        base = pl.multiple_of(step * dims.blk, 16)
        position = cube.position()
        works = []
        for n, (job_layer, job_half) in enumerate(jobs):
            blocks, inbox, send, recv = scatters[4 * n : 4 * n + 4]
            works.append(Scatter(groups[job_half], position, blocks, inbox, sums[n], send, recv))
        ticks = works[0].ticks

        def loads(n):
            job_layer, job_half = jobs[n]
            which = (1, 2) if job_half == ATTN else (0, 3, 4)
            return [
                pltpu.make_async_copy(whole_in[k].at[job_layer], kept[k].at[job_layer], load_sem.at[job_layer, k]) for k in which
            ]

        def begin():
            for n in range(len(jobs)):
                for copy in loads(n):
                    copy.start()
            qkv_ref[dims.blk :, :] = jnp.zeros_like(qkv_ref[dims.blk :, :])
            stream[...] = jnp.zeros_like(stream)
            wide_load(wide, og_ref)
            for image in range(dims.images):
                stream[image * dims.rows : image * dims.rows + dims.seq, :] = image_get(dims, wide, image) * alive(
                    live_ref, dims, image // dims.slots, image % dims.slots
                )
            greet(position[2] + [position[3]])

        def ready(n):
            for copy in loads(n):
                copy.wait()

        rider = Rider()
        rider.add(0, 0, begin)
        for n in range(len(jobs)):
            rider.add(n * steps, 0, lambda n=n: ready(n))
        end = (last, 2)
        for n, (job_layer, job_half) in enumerate(jobs):
            first = (n + 1) * steps
            if job_half == MLP:
                polls = [(first, 0), (first + 1, 0), (first + 2, 1), (first + 3, 1), (first + 4, 0), (first + 5, 0)]
            else:
                polls = [(first, 0), (first + 1, 0), (first + 2, 1), (first + 3, 1), (first + 4, 0), (first + 5, 0)]
            for t, (at, point) in enumerate(spread_ticks(ticks, polls)):
                if at <= last:
                    rider.add(at, point, lambda n=n, t=t: works[n].tick(t))
                else:
                    rider.add(*end, lambda n=n, t=t: works[n].tick(t))
        left = rider.due.pop(end)
        count = len(left) - ticks
        order = []
        for t in range(ticks):
            order += left[t : t + 1] if t < count else []
            order.append(left[count + t])
        rider.due[end] = order
        rider.at(index, 0)

        @pl.when(half == MLP)
        def _():
            def blocks(run):
                for n, (job_layer, job_half) in enumerate(jobs):
                    if job_half == MLP:

                        @pl.when(layer == job_layer)
                        def _(n=n):
                            run(scatters[4 * n])

            bwd_mlp_compute(
                dims, step, lambda: rider.at(index, 1, lambda at: (at // steps) % 2 == 0), vec_s.at[layer], w1_s.at[layer], w2_s.at[layer],
                mlp_in, work_scratch, groups[MLP], blocks,
            )

        @pl.when(half == ATTN)
        def _():
            def blocks(run):
                for n, (job_layer, job_half) in enumerate(jobs):
                    if job_half == ATTN:

                        @pl.when(layer == job_layer)
                        def _(n=n):
                            run(scatters[4 * n])

            bwd_attn_compute(
                dims, step, lambda: rider.at(index, 1, lambda at: (at // steps) % 2 == 1), vec_s.at[layer], wqkv_s.at[layer], wproj_s.at[layer],
                attn_in, work_scratch, groups[ATTN], blocks,
            )

        @pl.when(index > last - steps)
        def _():
            for g in range(PER_STEP):
                start = pl.multiple_of(base + g * dims.rows, 16)
                image_put(dims, wide, step * PER_STEP + g, stream[pl.ds(start, dims.seq), :])

        rider.at(index, 2)

    sem = DMA(Scatter.semaphores(cube))
    lead = lambda i: (LAYERS - 1 - i // (2 * steps)) * steps
    is_attn = lambda i: (i // steps) % 2
    attn_spec = lambda n: pl.BlockSpec((dims.blk, n), lambda i: (lead(i) + (i % steps) * is_attn(i), 0))
    mlp_spec = lambda n: pl.BlockSpec((dims.blk, n), lambda i: (lead(i) + (i % steps) * (1 - is_attn(i)) + (steps - 1) * is_attn(i), 0))
    whole_shapes = [w.shape for w in whole]
    outs = pl.pallas_call(
        body,
        grid=(last + 1,),
        in_specs=[SM, full(grad.shape)]
        + [ANY] * 5
        + [attn_spec(s.shape[1]) for s in saved_attn]
        + [mlp_spec(s.shape[1]) for s in saved_mlp],
        out_specs=[full(wide_shape(dims))] + [full(groups[h].block) for _, h in jobs],
        out_shape=[SDS(wide_shape(dims), F32)] + [SDS(groups[h].block, F32) for _, h in jobs],
        scratch_shapes=[
            pltpu.VMEM((tot, width), F32),
            pltpu.VMEM((2, tot, width), BF),
            pltpu.VMEM((tot, ff), BF),
            pltpu.VMEM((tot, ff), BF),
            pltpu.VMEM((VECS, ff), F32),
            pltpu.VMEM((VECS, LANES), F32),
            pltpu.VMEM((width, ff), BF),
            pltpu.VMEM((ff, width), BF),
            pltpu.VMEM((dims.blk + KEYS - dims.rows, 3 * width), BF),
            DMA((LAYERS, 5)),
        ]
        + [pltpu.VMEM(w.shape, w.dtype) for w in whole]
        + sum([[pltpu.VMEM(groups[h].buffer, BF), pltpu.VMEM(groups[h].buffer, BF), sem, sem] for _, h in jobs], []),
        compiler_params=params_of(1),
        name="backward",
    )(live, grad, *whole, *saved_attn, *saved_mlp)
    return outs[0], dict(zip(jobs, outs[1:]))


def emit_outputs(dims, groups, hidden, grad, sums, params):
    def body(*refs):
        (hidden_ref, grad_ref), blocks, (out_ref, in_grad_ref), outs = take(refs, 2, 2 * LAYERS, 2, 12)
        (n1g, n1b, wqkv, bqv, wproj, bpj, n2g, n2b, w1, bf1, w2, bf2) = outs
        weights = ([wqkv, wproj], [w1, w2])
        vectors = ((n1g, n1b, bpj, bqv, n2g, n2b, bf2, bf1), ())
        for c in range(hidden_ref.shape[0]):
            lanes = slice(c * LANES, (c + 1) * LANES)
            out_ref[:, lanes] = hidden_ref[c].astype(BF)
            in_grad_ref[:, lanes] = grad_ref[c]
        for layer in range(LAYERS):
            for half in (ATTN, MLP):
                groups[half].emit(layer, blocks[2 * layer + half], weights[half], vectors[half])

    return pl.pallas_call(
        body,
        in_specs=[VM] * (2 + 2 * LAYERS),
        out_specs=[VM] * 14,
        out_shape=[SDS((dims.flat, dims.width), BF), SDS((dims.flat, dims.width), F32)] + [SDS(p.shape, F32) for p in params],
        compiler_params=params_of(),
        name="emit",
    )(hidden, grad, *[sums[layer, half] for layer in range(LAYERS) for half in (ATTN, MLP)])


def per_device(devices, inputs, out_grad, live_counts, *params):
    cube = Cube(devices)
    images, seq, width = inputs.shape
    dims = Dims(images, live_counts.shape[0], seq, width, params[9].shape[1] * devices)
    size = lambda *which: [params[i].shape[1] for i in which]
    groups = [
        Group(cube, [params[2].shape[1:], params[4].shape[1:]], size(0, 1, 5, 3, 6, 7, 11, 9)),
        Group(cube, [params[8].shape[1:], params[10].shape[1:]], []),
    ]
    lay = lambda a: a.transpose(1, 0, 2).reshape(dims.flat, width)
    unlay = lambda a: a.reshape(seq, images, width).transpose(1, 0, 2)
    hidden, whole, saved_attn, saved_mlp = forward(cube, dims, groups, live_counts, lay(inputs), params)
    grad, sums = backward(cube, dims, groups, live_counts, lay(out_grad), whole, saved_attn, saved_mlp)
    outputs, in_grad, *grads = emit_outputs(dims, groups, hidden, grad, sums, params)
    return (unlay(outputs), unlay(in_grad), *grads)


def solution(mesh):
    devices = mesh.shape["fsdp"]
    rows3, flat2, rows2 = P("fsdp", None, None), P(None, "fsdp"), P(None, "fsdp", None)
    param_specs = (flat2, flat2, rows2, flat2, rows2, flat2, flat2, flat2, rows2, flat2, rows2, flat2)
    return jax.shard_map(
        functools.partial(per_device, devices),
        mesh=mesh,
        in_specs=(rows3, rows3, P("fsdp")) + param_specs,
        out_specs=(rows3, rows3) + param_specs,
        check_vma=False,
    )
```

profile of v0, /device:TPU:0, one launch (start us, length us, event | category | flops | bytes accessed | tf_op | source)
XLA Modules:
  0.0 220.5 jit_solution(5361768386689808680)
XLA Ops:
  0.6 1.3 copy.30.refs_6_
  2.0 1.5 copy.29.refs_4_
  3.4 1.5 copy.31.refs_10_
  5.0 93.2 %forward.1 = (f32[3,1576,128]{2,1,0:T(8,128)}, f32[2,8,1536]{2,1,0:T(8,128)}, bf16[2,384,1152]{2,1,0:T(8,128)(2,1)}, bf16[2,384,384]{2,1,0:T(8,128)(2,1)}, bf16[...) custom-call(s32[4]{0:T(128)} %refs_0_.3, ...), custom_call_target="tpu_custom_call" | custom-call | tf_op jit(solution)/shard_map/forward/pallas_call | solution.py:703
  98.2 112.8 %backward.1 = (f32[3,1576,128]{2,1,0:T(8,128)}, f32[2,144,128]{2,1,0:T(8,128)}, f32[2,80,128]{2,1,0:T(8,128)}, f32[2,144,128]{2,1,0:T(8,128)}, f32[2,80,128]{2,1,0:T(8,128)}) custom-call(s32[4]{0:T(128)} %refs_0_.3, bf16[1576,384]{1,0:T(8,128)(2,1)} %bitcast.13, f32[2,8,1536]{2,1,0:T(8,128)} %get-tuple-element.50.refs_2_, ...), custom_call_target="tpu_custom_call" | custom-call | tf_op jit(solution)/shard_map/backward/pallas_call | solution.py:848
  211.0 4.8 %emit.1 = (bf16[1576,384]{1,0:T(8,128)(2,1)}, f32[1576,384]{1,0:T(8,128)}, f32[2,12]{1,0:T(2,128)}, f32[2,12]{1,0:T(2,128)}, f32[2,12,1152]{2,1,0:T(8,128)}, /*i...) custom-call(f32[3,1576,128]{2,1,0:T(8,128)} %get-tuple-element.49.re, ...), custom_call_target="tpu_custom_call" | custom-call | tf_op jit(solution)/shard_map/emit/pallas_call | solution.py:891
  215.8 1.4 copy.33
  217.2 1.6 copy.32
  218.8 1.7 copy.34
where the time goes:
time: 221 us
  Pallas kernels  211 us (95%)
  local copies, waits for them, and re-layouts  9.07 us (4%)
    pallas_call x1, Pallas kernels, backward(): pl.pallas_call(body, grid=(last + 1,), in_specs=[SM, full(grad.shape)] +...  113 us
    pallas_call x1, Pallas kernels, forward(): pl.pallas_call(body, grid=(last + 1,), in_specs=[SM, full(x.shape)] + [fu...  93.2 us
    unnamed x6, local copies, waits for them, and re-layouts  9.07 us
    pallas_call x1, Pallas kernels, emit_outputs(): pl.pallas_call(body, in_specs=[VM] * (2 + 2 * LAYERS), out_specs=[VM] * 1...  4.76 us

commit v1 on v0

--- a/solution.py
+++ b/solution.py
@@ -112,7 +112,9 @@
     def pack_own(self, layer, weights, vectors, temp, store):
         for color, row, a, q, c in self.units:
             lanes = slice(c * LANES, (c + 1) * LANES)
-            store(color, row, row + self.rows, weights[a][layer, q * self.rows : (q + 1) * self.rows, lanes])
+            span = slice(q * self.rows, (q + 1) * self.rows)
+            at = (span, layer, lanes) if weights[a].shape[1] == LAYERS else (layer, span, lanes)
+            store(color, row, row + self.rows, weights[a][at])
         if self.sizes:
             for i, vector in enumerate(vectors):
                 temp[i : i + 1, : vector.shape[1]] = vector[layer : layer + 1, :].astype(F32)
@@ -177,7 +179,9 @@
     def emit(self, layer, block, weights, vectors):
         for color, row, a, q, c in self.units:
             lanes = slice(c * LANES, (c + 1) * LANES)
-            weights[a][layer, q * self.rows : (q + 1) * self.rows, lanes] = block[color, row : row + self.rows, :]
+            span = slice(q * self.rows, (q + 1) * self.rows)
+            at = (span, layer, lanes) if weights[a].shape[1] == LAYERS else (layer, span, lanes)
+            weights[a][at] = block[color, row : row + self.rows, :]
         for i, vector in enumerate(vectors):
             vector[layer : layer + 1, :] = block[0, self.vec_row + i : self.vec_row + i + 1, : vector.shape[1]]
 
@@ -619,16 +623,16 @@
             own[...] = jnp.zeros_like(own)
             groups[job_half].pack_own(job_layer, weights[job_half], vectors[job_half], temp, store)
 
-        def stage(t):
-            for n, work in enumerate(works):
-                if 0 <= t - n < ticks:
-                    if t == n:
-                        for copy in work.local(local_sem.at[n]):
-                            copy.start()
-                    if t - n == 1:
-                        for copy in work.local(local_sem.at[n]):
-                            copy.wait()
-                    work.tick(t - n)
+        begins = [0, 2] + [ticks - 1 + 2 * n for n in range(len(jobs) - 2)]
+
+        def tick(n, t):
+            if t == 0:
+                for copy in works[n].local(local_sem.at[n]):
+                    copy.start()
+            if t == 1:
+                for copy in works[n].local(local_sem.at[n]):
+                    copy.wait()
+            works[n].tick(t)
 
         def saves(n):
             job_layer, job_half = jobs[n]
@@ -651,9 +655,11 @@
             pack(0)
             greet(position[2] + [position[3]])
             for t in range(ticks):
-                if 0 < t < len(jobs):
-                    pack(t)
-                stage(t)
+                for n in range(len(jobs)):
+                    if 0 <= t - begins[n] < ticks:
+                        tick(n, t - begins[n])
+                if t + 1 < len(jobs):
+                    pack(t + 1)
                 if t == 2:
                     qkv_ref[dims.blk :, :] = jnp.zeros_like(qkv_ref[dims.blk :, :])
                     stream[...] = jnp.zeros_like(stream)
@@ -664,8 +670,15 @@
 
         rider = Rider()
         rider.add(0, 0, begin)
-        for late in range(1, len(jobs)):
-            rider.add(min(late, steps - 1), 0, lambda late=late: stage(ticks + late - 1))
+        timed = [(), (0, 0, 0, 0, 3, 4), (0, 1, 2, 3, 5, 7), (2, 4, 6, 8, 11, 12)]
+        for late in range(ticks, begins[-1] + ticks):
+            at = late - ticks + 1
+            at += at // steps
+            for n in range(1, len(jobs)):
+                if 0 <= late - begins[n] < ticks:
+                    t = late - begins[n]
+                    poll = timed[n][t] if ticks == 6 and steps == 4 and n < len(timed) else at
+                    rider.add(min(poll, n * steps), 0, lambda n=n, t=t: tick(n, t))
         for n in range(1, len(jobs)):
             rider.add(n * steps, 0, lambda n=n: finish(n))
         rider.at(index, 0)
@@ -909,10 +922,12 @@
     ]
     lay = lambda a: a.transpose(1, 0, 2).reshape(dims.flat, width)
     unlay = lambda a: a.reshape(seq, images, width).transpose(1, 0, 2)
-    hidden, whole, saved_attn, saved_mlp = forward(cube, dims, groups, live_counts, lay(inputs), params)
+    turn = lambda a: a.transpose(1, 0, 2) if a.ndim == 3 and a.shape[1 if a.shape[0] == LAYERS else 0] % 8 else a
+    turned = [turn(p) for p in params]
+    hidden, whole, saved_attn, saved_mlp = forward(cube, dims, groups, live_counts, lay(inputs), turned)
     grad, sums = backward(cube, dims, groups, live_counts, lay(out_grad), whole, saved_attn, saved_mlp)
-    outputs, in_grad, *grads = emit_outputs(dims, groups, hidden, grad, sums, params)
-    return (unlay(outputs), unlay(in_grad), *grads)
+    outputs, in_grad, *grads = emit_outputs(dims, groups, hidden, grad, sums, turned)
+    return (unlay(outputs), unlay(in_grad), *[turn(g) for g in grads])
 
 
 def solution(mesh):

time: 221 us -> 199 us (0.900)
  Pallas kernels: 211 us -> 198 us
  local copies, waits for them, and re-layouts: 9.07 us -> 0 us
    pallas_call x1, Pallas kernels: 93.2 us -> 82.2 us  [forward(): pl.pallas_call(body, grid=(last + 1,), in_specs=[SM, full(x.shape)] + [fu...]
    unnamed x6 -> x0, local copies, waits for them, and re-layouts: 9.07 us -> none
where the time goes in v1:
time: 199 us
  Pallas kernels  198 us (99%)
    pallas_call x1, Pallas kernels, backward(): pl.pallas_call(body, grid=(last + 1,), in_specs=[SM, full(grad.shape)] +...  111 us
    pallas_call x1, Pallas kernels, forward(): pl.pallas_call(body, grid=(last + 1,), in_specs=[SM, full(x.shape)] + [fu...  82.2 us
    pallas_call x1, Pallas kernels, emit_outputs(): pl.pallas_call(body, in_specs=[VM] * (2 + 2 * LAYERS), out_specs=[VM] * 1...  4.82 us

profile of v1, /device:TPU:0, one launch (start us, length us, event | category | flops | bytes accessed | tf_op | source)
XLA Modules:
  0.0 199.2 jit_solution(3037810594309031466)
XLA Ops:
  0.7 82.2 %forward.1 = (f32[3,1576,128]{2,1,0:T(8,128)}, f32[2,8,1536]{2,1,0:T(8,128)}, bf16[2,384,1152]{2,1,0:T(8,128)(2,1)}, bf16[2,384,384]{2,1,0:T(8,128)(2,1)}, bf16[...) custom-call(s32[4]{0:T(128)} %refs_0_.3, ...), custom_call_target="tpu_custom_call" | custom-call | tf_op jit(solution)/shard_map/forward/pallas_call | solution.py:716
  82.9 111.4 %backward.1 = (f32[3,1576,128]{2,1,0:T(8,128)}, f32[2,144,128]{2,1,0:T(8,128)}, f32[2,80,128]{2,1,0:T(8,128)}, f32[2,144,128]{2,1,0:T(8,128)}, f32[2,80,128]{2,1,0:T(8,128)}) custom-call(s32[4]{0:T(128)} %refs_0_.3, bf16[1576,384]{1,0:T(8,128)(2,1)} %bitcast.19, f32[2,8,1536]{2,1,0:T(8,128)} %get-tuple-element.50.refs_2_, ...), custom_call_target="tpu_custom_call" | custom-call | tf_op jit(solution)/shard_map/backward/pallas_call | solution.py:861
  194.2 4.8 %emit.1 = (bf16[1576,384]{1,0:T(8,128)(2,1)}, f32[1576,384]{1,0:T(8,128)}, f32[2,12]{1,0:T(2,128)}, f32[2,12]{1,0:T(2,128)}, f32[12,2,1152]{2,1,0:T(2,128)}, /*i...) custom-call(f32[3,1576,128]{2,1,0:T(8,128)} %get-tuple-element.49.re, ...), custom_call_target="tpu_custom_call" | custom-call | tf_op jit(solution)/shard_map/emit/pallas_call | solution.py:904

commit v2 on v1

--- a/solution.py
+++ b/solution.py
@@ -809,8 +809,8 @@
         count = len(left) - ticks
         order = []
         for t in range(ticks):
+            order.append(left[count + t])
             order += left[t : t + 1] if t < count else []
-            order.append(left[count + t])
         rider.due[end] = order
         rider.at(index, 0)
 

time: 199 us -> 197 us (0.990)
  Pallas kernels: 198 us -> 196 us
    pallas_call x1, Pallas kernels: 111 us -> 109 us  [backward(): pl.pallas_call(body, grid=(last + 1,), in_specs=[SM, full(grad.shape)] +...]
where the time goes in v2:
time: 197 us
  Pallas kernels  196 us (99%)
    pallas_call x1, Pallas kernels, backward(): pl.pallas_call(body, grid=(last + 1,), in_specs=[SM, full(grad.shape)] +...  109 us
    pallas_call x1, Pallas kernels, forward(): pl.pallas_call(body, grid=(last + 1,), in_specs=[SM, full(x.shape)] + [fu...  82.2 us
    pallas_call x1, Pallas kernels, emit_outputs(): pl.pallas_call(body, in_specs=[VM] * (2 + 2 * LAYERS), out_specs=[VM] * 1...  4.82 us

profile of v2, /device:TPU:0, one launch (start us, length us, event | category | flops | bytes accessed | tf_op | source)
XLA Modules:
  0.0 196.9 jit_solution(129089365938436451)
XLA Ops:
  0.7 82.2 %forward.1 = (f32[3,1576,128]{2,1,0:T(8,128)}, f32[2,8,1536]{2,1,0:T(8,128)}, bf16[2,384,1152]{2,1,0:T(8,128)(2,1)}, bf16[2,384,384]{2,1,0:T(8,128)(2,1)}, bf16[...) custom-call(s32[4]{0:T(128)} %refs_0_.3, ...), custom_call_target="tpu_custom_call" | custom-call | tf_op jit(solution)/shard_map/forward/pallas_call | solution.py:716
  82.9 109.1 %backward.1 = (f32[3,1576,128]{2,1,0:T(8,128)}, f32[2,144,128]{2,1,0:T(8,128)}, f32[2,80,128]{2,1,0:T(8,128)}, f32[2,144,128]{2,1,0:T(8,128)}, f32[2,80,128]{2,1,0:T(8,128)}) custom-call(s32[4]{0:T(128)} %refs_0_.3, bf16[1576,384]{1,0:T(8,128)(2,1)} %bitcast.19, f32[2,8,1536]{2,1,0:T(8,128)} %get-tuple-element.50.refs_2_, ...), custom_call_target="tpu_custom_call" | custom-call | tf_op jit(solution)/shard_map/backward/pallas_call | solution.py:861
  191.9 4.8 %emit.1 = (bf16[1576,384]{1,0:T(8,128)(2,1)}, f32[1576,384]{1,0:T(8,128)}, f32[2,12]{1,0:T(2,128)}, f32[2,12]{1,0:T(2,128)}, f32[12,2,1152]{2,1,0:T(2,128)}, /*i...) custom-call(f32[3,1576,128]{2,1,0:T(8,128)} %get-tuple-element.49.re, ...), custom_call_target="tpu_custom_call" | custom-call | tf_op jit(solution)/shard_map/emit/pallas_call | solution.py:904
